TPU v7x, 32 devices: a whole 2x2x4 slice. The times are simulated.
32 devices in a mesh: dp: 8 (over z, core), seq: 4 (over y, x).
Axes of the slice: x: 2, y: 2, z: 4, core: 2. Of those that a mesh axis runs over, the one named last changes fastest.
Arguments:
- tokens: bfloat16 [2, 8, 512, 768], P(None, 'dp', 'seq'), may hold values from -6 to 6
- piece_starts: int32 [2, 8, 2], P(None, 'dp'), may hold values from 0 to 256, as said below
- qkv_weight: bfloat16 [768, 2304], P(('dp', 'seq')), may hold values from -0.21875 to 0.21875
- qv_bias: bfloat16 [1536], P(('dp', 'seq')), may hold values from -1.796875 to 1.796875
- out_weight: bfloat16 [768, 768], P(('dp', 'seq')), may hold values from -1.25 to 1.25
- out_bias: bfloat16 [768], P(('dp', 'seq')), may hold values from -1.796875 to 1.796875
- norm1_gain: bfloat16 [768], P(('dp', 'seq')), may hold values from 0.5 to 1.5
- norm1_bias: bfloat16 [768], P(('dp', 'seq')), may hold values from -1.796875 to 1.796875
- up_weight: bfloat16 [768, 3072], P(('dp', 'seq')), may hold values from -0.21875 to 0.21875
- up_bias: bfloat16 [3072], P(('dp', 'seq')), may hold values from -1.796875 to 1.796875
- down_weight: bfloat16 [3072, 768], P(('dp', 'seq')), may hold values from -0.109375 to 0.109375
- down_bias: bfloat16 [768], P(('dp', 'seq')), may hold values from -1.796875 to 1.796875
- norm2_gain: bfloat16 [768], P(('dp', 'seq')), may hold values from 0.5 to 1.5
- norm2_bias: bfloat16 [768], P(('dp', 'seq')), may hold values from -1.796875 to 1.796875
- grad_out: bfloat16 [2, 8, 512, 768], P(None, 'dp', 'seq'), may hold values from -6 to 6
Outputs:
- layer_out: bfloat16 [2, 8, 512, 768], P(None, 'dp', 'seq')
- tokens_grad: float32 [2, 8, 512, 768], P(None, 'dp', 'seq')
- qkv_weight_grad: float32 [768, 2304], P(('dp', 'seq'))
- qv_bias_grad: float32 [1536], P(('dp', 'seq'))
- out_weight_grad: float32 [768, 768], P(('dp', 'seq'))
- out_bias_grad: float32 [768], P(('dp', 'seq'))
- norm1_gain_grad: float32 [768], P(('dp', 'seq'))
- norm1_bias_grad: float32 [768], P(('dp', 'seq'))
- up_weight_grad: float32 [768, 3072], P(('dp', 'seq'))
- up_bias_grad: float32 [3072], P(('dp', 'seq'))
- down_weight_grad: float32 [3072, 768], P(('dp', 'seq'))
- down_bias_grad: float32 [768], P(('dp', 'seq'))
- norm2_gain_grad: float32 [768], P(('dp', 'seq'))
- norm2_bias_grad: float32 [768], P(('dp', 'seq'))
Inputs may be any that keep to these rules, and one draw needn't show every extreme that they name: `piece_starts`: each sequence's 2 pieces of 256 positions lie inside it, in rising order, without intersection.
All inputs are finite; a program needn't handle non-finite values.
Results may differ from a plain program's by a relative error of at most 0.018.
Values may be sent and summed in bfloat16 or wider, within the bound.
A program may use at most 192 MiB of HBM per device.

v0:
```python
import math
import jax
import jax.numpy as jnp
from jax import lax
from jax.sharding import PartitionSpec as P

HEADS = 12
PIC = 256
NEG = -1e30
EPS = 1e-05


def owners(positions, starts):
    inside = (positions[:, None] >= starts[None, :]) & (positions[:, None] < starts[None, :] + PIC)
    return jnp.max(jnp.where(inside, starts[None, :], -1), axis=1)


def visible_mask(query_pos, query_owner, key_pos, key_owner):
    later = key_pos[None, :] <= query_pos[:, None]
    shared = (key_owner[None, :] == query_owner[:, None]) & (query_owner[:, None] >= 0)
    return later | shared


def normalize(values):
    centre = values - jnp.mean(values, axis=-1, keepdims=True)
    inverse = lax.rsqrt(jnp.mean(centre * centre, axis=-1, keepdims=True) + EPS)
    return (centre * inverse, inverse)


def norm_back(upstream, normed, inverse, gain):
    scaled = upstream * gain
    return inverse * (
        scaled
        - jnp.mean(scaled, axis=-1, keepdims=True)
        - normed * jnp.mean(scaled * normed, axis=-1, keepdims=True)
    )


def matmul(left, right):
    return jnp.dot(left, right, preferred_element_type=jnp.float32)


def left_trans(left, right):
    return lax.dot_general(
        left, right, (((0,), (0,)), ((), ())), preferred_element_type=jnp.float32
    )


def right_trans(left, right):
    return lax.dot_general(
        left, right, (((1,), (1,)), ((), ())), preferred_element_type=jnp.float32
    )


def key_blocks(count):
    size = math.gcd(count, 1024)
    return (size, count // size)


def gather_forward(shards):
    return (
        lax.all_gather(shards[0], ("dp", "seq"), axis=0, tiled=True),
        lax.all_gather(shards[1], ("dp", "seq"), axis=0, tiled=True),
        lax.all_gather(shards[2], ("dp", "seq"), axis=0, tiled=True),
        lax.all_gather(shards[3], ("dp", "seq"), axis=0, tiled=True),
        lax.all_gather(shards[4], ("dp", "seq"), axis=0, tiled=True),
        lax.all_gather(shards[5], ("dp", "seq"), axis=0, tiled=True),
        lax.all_gather(shards[6], ("dp", "seq"), axis=0, tiled=True),
        lax.all_gather(shards[7], ("dp", "seq"), axis=0, tiled=True),
        lax.all_gather(shards[8], ("dp", "seq"), axis=0, tiled=True),
        lax.all_gather(shards[9], ("dp", "seq"), axis=0, tiled=True),
        lax.all_gather(shards[10], ("dp", "seq"), axis=0, tiled=True),
        lax.all_gather(shards[11], ("dp", "seq"), axis=0, tiled=True),
    )


def gather_backward(shards):
    return (
        lax.all_gather(shards[0], ("dp", "seq"), axis=0, tiled=True),
        lax.all_gather(shards[1], ("dp", "seq"), axis=0, tiled=True),
        lax.all_gather(shards[2], ("dp", "seq"), axis=0, tiled=True),
        lax.all_gather(shards[3], ("dp", "seq"), axis=0, tiled=True),
        lax.all_gather(shards[4], ("dp", "seq"), axis=0, tiled=True),
        lax.all_gather(shards[5], ("dp", "seq"), axis=0, tiled=True),
        lax.all_gather(shards[6], ("dp", "seq"), axis=0, tiled=True),
        lax.all_gather(shards[7], ("dp", "seq"), axis=0, tiled=True),
        lax.all_gather(shards[8], ("dp", "seq"), axis=0, tiled=True),
        lax.all_gather(shards[9], ("dp", "seq"), axis=0, tiled=True),
        lax.all_gather(shards[10], ("dp", "seq"), axis=0, tiled=True),
        lax.all_gather(shards[11], ("dp", "seq"), axis=0, tiled=True),
    )


def column_sum(values):
    return jnp.sum(values.astype(jnp.float32), axis=0)


def on_device(
    tokens,
    piece_starts,
    qkv_weight,
    qv_bias,
    out_weight,
    out_bias,
    norm1_gain,
    norm1_bias,
    up_weight,
    up_bias,
    down_weight,
    down_bias,
    norm2_gain,
    norm2_bias,
    grad_out,
):
    shards = (
        qkv_weight,
        qv_bias,
        out_weight,
        out_bias,
        norm1_gain,
        norm1_bias,
        up_weight,
        up_bias,
        down_weight,
        down_bias,
        norm2_gain,
        norm2_bias,
    )
    micro_count = tokens.shape[0]
    rows = tokens.shape[2]
    width = tokens.shape[3]
    head_size = width // HEADS
    scale = 1.0 / math.sqrt(head_size)
    length = rows * lax.axis_size("seq")
    query_pos = lax.axis_index("seq") * rows + jnp.arange(rows, dtype=jnp.int32)
    totals = None
    outputs = []
    input_grads = []
    for micro in range(micro_count):
        params = gather_forward(shards)
        (
            full_qkv,
            full_qvb,
            full_out,
            full_outb,
            full_g1,
            full_b1,
            full_up,
            full_upb,
            full_down,
            full_downb,
            full_g2,
            full_b2,
        ) = params
        starts = piece_starts[micro, 0]
        query_owner = owners(query_pos, starts)
        source = tokens[micro, 0]
        joined = matmul(source, full_qkv)
        queries = (joined[:, :width] + full_qvb[:width].astype(jnp.float32)).astype(jnp.bfloat16)
        keys = joined[:, width : 2 * width].astype(jnp.bfloat16)
        values = (joined[:, 2 * width :] + full_qvb[width:].astype(jnp.float32)).astype(
            jnp.bfloat16
        )
        query_heads = queries.reshape(rows, HEADS, head_size)

        def block_scores(key_block, key_pos):
            scores = (
                jnp.einsum(
                    "qhd,khd->hqk", query_heads, key_block, preferred_element_type=jnp.float32
                )
                * scale
            )
            allowed = visible_mask(query_pos, query_owner, key_pos, owners(key_pos, starts))
            return jnp.where(allowed[None], scores, NEG)

        initial = (
            jnp.full((HEADS, rows), NEG, jnp.float32),
            jnp.zeros((HEADS, rows), jnp.float32),
            jnp.zeros((HEADS, rows, head_size), jnp.float32),
        )
        key_piece = lax.all_gather(keys, "seq", axis=0, tiled=True)
        value_piece = lax.all_gather(values, "seq", axis=0, tiled=True)
        size, count = key_blocks(key_piece.shape[0])

        def one(block, carry):
            run_max, total, accum = carry
            key_block = lax.dynamic_slice_in_dim(key_piece, block * size, size, 0).reshape(
                size, HEADS, head_size
            )
            value_block = lax.dynamic_slice_in_dim(value_piece, block * size, size, 0).reshape(
                size, HEADS, head_size
            )
            key_pos = block * size + jnp.arange(size, dtype=jnp.int32)
            scores = block_scores(key_block, key_pos)
            new_max = jnp.maximum(run_max, jnp.max(scores, axis=-1))
            factor = jnp.exp(run_max - new_max)
            weights = jnp.exp(scores - new_max[:, :, None])
            total = total * factor + jnp.sum(weights, axis=-1)
            accum = accum * factor[:, :, None] + jnp.einsum(
                "hqk,khd->hqd",
                weights.astype(jnp.bfloat16),
                value_block,
                preferred_element_type=jnp.float32,
            )
            return (new_max, total, accum)

        run_max, total, accum = lax.fori_loop(0, count, one, initial)
        lse = run_max + jnp.log(total)
        exact = (accum / total[:, :, None]).transpose(1, 0, 2)
        attended = exact.reshape(rows, width).astype(jnp.bfloat16)
        resid1 = (
            source.astype(jnp.float32) + matmul(attended, full_out) + full_outb.astype(jnp.float32)
        )
        normed1, inverse1 = normalize(resid1)
        gain1 = full_g1.astype(jnp.float32)
        mixed1 = normed1 * gain1 + full_b1.astype(jnp.float32)
        inner = mixed1.astype(jnp.bfloat16)
        pre = matmul(inner, full_up) + full_upb.astype(jnp.float32)
        act = jax.nn.gelu(pre, approximate=False).astype(jnp.bfloat16)
        resid2 = mixed1 + matmul(act, full_down) + full_downb.astype(jnp.float32)
        normed2, inverse2 = normalize(resid2)
        gain2 = full_g2.astype(jnp.float32)
        outputs.append((normed2 * gain2 + full_b2.astype(jnp.float32)).astype(jnp.bfloat16))
        back = gather_backward(shards)
        back_qkv = back[0]
        back_out = back[2]
        back_up = back[6]
        back_down = back[8]
        cotan = grad_out[micro, 0].astype(jnp.float32)
        d_resid2 = norm_back(cotan, normed2, inverse2, gain2)
        grad_g2 = jnp.sum(cotan * normed2, axis=0)
        grad_b2 = jnp.sum(cotan, axis=0)
        d_branch2 = d_resid2.astype(jnp.bfloat16)
        grad_downb = column_sum(d_branch2)
        grad_down = left_trans(act, d_branch2)
        d_act = right_trans(d_branch2, back_down)
        gelu_value, gelu_back = jax.vjp(lambda value: jax.nn.gelu(value, approximate=False), pre)
        d_pre = gelu_back(d_act)[0].astype(jnp.bfloat16)
        grad_upb = column_sum(d_pre)
        grad_up = left_trans(inner, d_pre)
        d_mixed1 = d_resid2 + right_trans(d_pre, back_up)
        d_resid1 = norm_back(d_mixed1, normed1, inverse1, gain1)
        grad_g1 = jnp.sum(d_mixed1 * normed1, axis=0)
        grad_b1 = jnp.sum(d_mixed1, axis=0)
        d_branch1 = d_resid1.astype(jnp.bfloat16)
        grad_outb = column_sum(d_branch1)
        grad_out_w = left_trans(attended, d_branch1)
        d_attended = right_trans(d_branch1, back_out).astype(jnp.bfloat16)
        grad_heads = d_attended.reshape(rows, HEADS, head_size)
        delta = jnp.sum(grad_heads.astype(jnp.float32) * exact, axis=-1).T
        initial_back = (
            jnp.zeros((rows, HEADS, head_size), jnp.float32),
            jnp.zeros((length, width), jnp.float32),
            jnp.zeros((length, width), jnp.float32),
        )
        fold_key_piece = lax.all_gather(keys, "seq", axis=0, tiled=True)
        fold_value_piece = lax.all_gather(values, "seq", axis=0, tiled=True)
        fold_size, fold_count = key_blocks(fold_key_piece.shape[0])

        def fold_one(block, carry):
            query_grad, key_grads, value_grads = carry
            offset = block * fold_size
            key_block = lax.dynamic_slice_in_dim(fold_key_piece, offset, fold_size, 0).reshape(
                fold_size, HEADS, head_size
            )
            value_block = lax.dynamic_slice_in_dim(fold_value_piece, offset, fold_size, 0).reshape(
                fold_size, HEADS, head_size
            )
            key_pos = offset + jnp.arange(fold_size, dtype=jnp.int32)
            probs = jnp.exp(block_scores(key_block, key_pos) - lse[:, :, None])
            d_probs = jnp.einsum(
                "qhd,khd->hqk", grad_heads, value_block, preferred_element_type=jnp.float32
            )
            d_scores = (probs * (d_probs - delta[:, :, None])).astype(jnp.bfloat16)
            query_grad = (
                query_grad
                + jnp.einsum(
                    "hqk,khd->qhd", d_scores, key_block, preferred_element_type=jnp.float32
                )
                * scale
            )
            key_part = (
                jnp.einsum(
                    "hqk,qhd->khd", d_scores, query_heads, preferred_element_type=jnp.float32
                ).reshape(fold_size, width)
                * scale
            )
            value_part = jnp.einsum(
                "hqk,qhd->khd",
                probs.astype(jnp.bfloat16),
                grad_heads,
                preferred_element_type=jnp.float32,
            ).reshape(fold_size, width)
            key_grads = lax.dynamic_update_slice_in_dim(
                key_grads,
                lax.dynamic_slice_in_dim(key_grads, offset, fold_size, 0) + key_part,
                offset,
                0,
            )
            value_grads = lax.dynamic_update_slice_in_dim(
                value_grads,
                lax.dynamic_slice_in_dim(value_grads, offset, fold_size, 0) + value_part,
                offset,
                0,
            )
            return (query_grad, key_grads, value_grads)

        query_grad, key_grads, value_grads = lax.fori_loop(0, fold_count, fold_one, initial_back)
        key_grad, value_grad = (
            lax.psum_scatter(
                key_grads.astype(jnp.bfloat16), "seq", scatter_dimension=0, tiled=True
            ).astype(jnp.float32),
            lax.psum_scatter(
                value_grads.astype(jnp.bfloat16), "seq", scatter_dimension=0, tiled=True
            ).astype(jnp.float32),
        )
        query_share = query_grad.reshape(rows, width)
        d_queries = query_share.astype(jnp.bfloat16)
        d_keys = key_grad.astype(jnp.bfloat16)
        d_values = value_grad.astype(jnp.bfloat16)
        d_joined = jnp.concatenate([d_queries, d_keys, d_values], axis=1)
        grad_qvb = jnp.concatenate([column_sum(d_queries), column_sum(d_values)], axis=0)
        grad_qkv = left_trans(source, d_joined)
        input_grads.append(d_resid1 + right_trans(d_joined, back_qkv))
        terms = (
            grad_qkv,
            grad_qvb,
            grad_out_w,
            grad_outb,
            grad_g1,
            grad_b1,
            grad_up,
            grad_upb,
            grad_down,
            grad_downb,
            grad_g2,
            grad_b2,
        )
        if totals is None:
            totals = terms
        else:
            totals = tuple((first + second for first, second in zip(totals, terms)))
    shares = lax.psum_scatter(totals, ("dp", "seq"), scatter_dimension=0, tiled=True)
    layer_out = jnp.stack(outputs)[:, None]
    tokens_grad = jnp.stack(input_grads)[:, None]
    return (
        layer_out,
        tokens_grad,
        shares[0],
        shares[1],
        shares[2],
        shares[3],
        shares[4],
        shares[5],
        shares[6],
        shares[7],
        shares[8],
        shares[9],
        shares[10],
        shares[11],
    )


def solution(mesh):
    return jax.shard_map(
        on_device,
        mesh=mesh,
        in_specs=(
            P(None, "dp", "seq", None),
            P(None, "dp", None),
            P(("dp", "seq"), None),
            P(("dp", "seq")),
            P(("dp", "seq"), None),
            P(("dp", "seq")),
            P(("dp", "seq")),
            P(("dp", "seq")),
            P(("dp", "seq"), None),
            P(("dp", "seq")),
            P(("dp", "seq"), None),
            P(("dp", "seq")),
            P(("dp", "seq")),
            P(("dp", "seq")),
            P(None, "dp", "seq", None),
        ),
        out_specs=(
            P(None, "dp", "seq", None),
            P(None, "dp", "seq", None),
            P(("dp", "seq"), None),
            P(("dp", "seq")),
            P(("dp", "seq"), None),
            P(("dp", "seq")),
            P(("dp", "seq")),
            P(("dp", "seq")),
            P(("dp", "seq"), None),
            P(("dp", "seq")),
            P(("dp", "seq"), None),
            P(("dp", "seq")),
            P(("dp", "seq")),
            P(("dp", "seq")),
        ),
        check_vma=False,
    )
```

profile of v0, /device:TPU:0, one launch (start us, length us, event | category | flops | bytes accessed | tf_op | source)
XLA Modules:
  0.0 927.6 jit_solution(920579388821818816)
XLA Ops:
  16.8 42.6 %all-reduce.17 = (bf16[3072]{0:T(1024)(128)(2,1)S(1)}, bf16[1536]{0:T(1024)(128)(2,1)S(1)}, bf16[768]{0:T(1024)(128)(2,1)S(1)}, bf16[768]{0:T(1024)(128)(2,1)S(1...) all-reduce(bf16[3072]{0:T(1024)(128)(2,1)S(1)} %dynamic-update-slic, ...), channel_id=1, replica_groups=mesh['dp'=8,'seq'=4] {'dp','seq'}, use_global_device_ids=true, to_apply=%add.4 | all-reduce | flops 9216 | bytes 36864
  64.7 8.9 all-gather.5.cloned.1.call-done
  73.6 2.9 fusion.95
  77.7 12.7 %all_gather.34 = bf16[512,768]{1,0:T(8,128)(2,1)S(1)} all-gather(bf16[128,768]{1,0:T(8,128)(2,1)S(1)} %slice.119), channel_id=1, replica_groups=mesh['dp'=8,'seq'=4] {'seq'}, dimensions={0}, use_global_device_ids=true | all-gather | bytes 983040 | tf_op jit(solution)/shard_map/all_gather | solution.py:181
  91.6 10.5 %all_gather.35 = bf16[512,768]{1,0:T(8,128)(2,1)S(1)} all-gather(bf16[128,768]{1,0:T(8,128)(2,1)S(1)} %get-tuple-element.277), channel_id=1, replica_groups=mesh['dp'=8,'seq'=4] {'seq'}, dimensions={0}, use_global_device_ids=true | all-gather | bytes 983040 | tf_op jit(solution)/shard_map/all_gather | solution.py:182
  104.0 12.6 %all_gather.86 = bf16[512,768]{1,0:T(8,128)(2,1)S(1)} all-gather(bf16[128,768]{1,0:T(8,128)(2,1)S(1)} %slice.118), channel_id=1, replica_groups=mesh['dp'=8,'seq'=4] {'seq'}, dimensions={0}, use_global_device_ids=true | all-gather | bytes 983040 | tf_op jit(solution)/shard_map/all_gather | solution.py:181
  117.8 10.7 %all_gather.87 = bf16[512,768]{1,0:T(8,128)(2,1)S(1)} all-gather(bf16[128,768]{1,0:T(8,128)(2,1)S(1)} %get-tuple-element.271), channel_id=1, replica_groups=mesh['dp'=8,'seq'=4] {'seq'}, dimensions={0}, use_global_device_ids=true | all-gather | bytes 983040 | tf_op jit(solution)/shard_map/all_gather | solution.py:182
  143.2 52.6 %all-gather.9.cloned.1.call-done = bf16[768,3072]{1,0:T(8,128)(2,1)} async-done(((bf16[24,3072]{1,0:T(8,128)(2,1)}), bf16[768,3072]{1,0:T(8,128)(2,1)}) %all-gather.9.cloned.1.call-update) | async-done | bytes 4718608 | tf_op jit(solution)/shard_map/all_gather | solution.py:68
  195.8 8.7 multiply_convert_fusion.5
  204.5 55.9 %all-gather.11.cloned.1.call-done = bf16[3072,768]{1,0:T(8,128)(2,1)} async-done(((bf16[96,768]{1,0:T(8,128)(2,1)}), bf16[3072,768]{1,0:T(8,128)(2,1)}) %all-gather.11.cloned.1.call-update) | async-done | bytes 4718608 | tf_op jit(solution)/shard_map/all_gather | solution.py:70
  260.4 3.6 fusion.139
  264.5 5.5 multiply_convert_fusion.4
  278.8 2.5 convert_reduce_fusion
  281.3 3.1 convert_reduce_fusion.7
  289.1 3.6 fusion.33
  296.2 3.1 multiply_convert_fusion
  304.1 2.7 convolution_convert_fusion.1
  308.5 2.6 fusion.30
  323.9 2.5 convert_reduce_fusion.9
  328.9 19.7 %reduce-scatter.29.cloned.1.call-done = bf16[128,768]{1,0:T(8,128)(2,1)} async-done(((bf16[512,768]{1,0:T(8,128)(2,1)}), bf16[128,768]{1,0:T(8,128)(2,1)}) %reduce-scatter.29.cloned.1.call-update) | async-done | bytes 196624
  349.7 28.0 %reduce-scatter.27.cloned.1.call-done = bf16[128,768]{1,0:T(8,128)(2,1)} async-done(((bf16[512,768]{1,0:T(8,128)(2,1)}), bf16[128,768]{1,0:T(8,128)(2,1)}) %reduce-scatter.27.cloned.1.call-update) | async-done | bytes 196624
  378.8 28.0 %reduce-scatter.25.cloned.1.call-done = bf16[128,768]{1,0:T(8,128)(2,1)} async-done(((bf16[512,768]{1,0:T(8,128)(2,1)}), bf16[128,768]{1,0:T(8,128)(2,1)}) %reduce-scatter.25.cloned.1.call-update) | async-done | bytes 196624
  409.0 4.0 add_bitcast_fusion
  413.0 8.0 copy.87
  423.7 5.1 convolution_add_fusion.1
  431.6 5.1 convolution_add_fusion
  451.6 41.7 %all-reduce.16 = (f32[1536]{0:T(1024)}, f32[768]{0:T(1024)}, f32[768]{0:T(1024)}, f32[768]{0:T(1024)}, f32[3072]{0:T(1024)}, /*index=5*/f32[768]{0:T(1024)}, f32[768]{0:T(1024)}, f32[768]{0:T(1024)}) all-reduce(f32[1536]{0:T(1024)} %maximum_add_fusion, f32[768]{0:T(1024)S(1)} %add.424, ...), channel_id=7, replica_groups=mesh['dp'=8,'seq'=4] {'dp','seq'}, use_global_device_ids=true, to_apply=%region_35.36.clone | all-reduce | flops 9216 | bytes 73728
  503.5 2.6 fusion.56
  508.4 4.1 reduce-scatter.19.cloned.1.call-done
  512.5 124.8 %reduce-scatter.33.cloned.1.call-done = f32[24,2304]{1,0:T(8,128)} async-done(((f32[768,2304]{1,0:T(8,128)}), f32[24,2304]{1,0:T(8,128)}) %reduce-scatter.33.cloned.1.call-update) | async-done | bytes 221200
  637.3 141.6 %reduce-scatter.21.cloned.1.call-done = f32[24,3072]{1,0:T(8,128)} async-done(((f32[768,3072]{1,0:T(8,128)}), f32[24,3072]{1,0:T(8,128)}) %reduce-scatter.21.cloned.1.call-update) | async-done | bytes 294928 | tf_op jit(solution)/shard_map/reduce_scatter | solution.py:343
  778.9 141.5 %reduce-scatter.23.cloned.1.call-done = f32[96,768]{1,0:T(8,128)} async-done(((f32[3072,768]{1,0:T(8,128)}), f32[96,768]{1,0:T(8,128)}) %reduce-scatter.23.cloned.1.call-update) | async-done | bytes 294928 | tf_op jit(solution)/shard_map/reduce_scatter | solution.py:343
  (298 shorter events, 110.7 us)
Async XLA Ops:
  7.2 66.4 %all-gather.5.cloned.1.call-start = ((), (), s32[]{:S(2)}) async-start(), calls=%async_computation.8 | async-start | bytes 3649536 | tf_op jit(solution)/shard_map/all_gather | solution.py:62
  7.9 126.4 %all-gather.7.cloned.1.call-start = ((), (), s32[]{:S(2)}) async-start(), calls=%async_computation.9 | async-start | bytes 1216512 | tf_op jit(solution)/shard_map/all_gather | solution.py:64
  8.7 187.2 %all-gather.9.cloned.1.call-start = ((), (), s32[]{:S(2)}) async-start(), calls=%async_computation.10 | async-start | bytes 4866048 | tf_op jit(solution)/shard_map/all_gather | solution.py:68
  9.4 251.0 %all-gather.11.cloned.1.call-start = ((), (), s32[]{:S(2)}) async-start(), calls=%async_computation.11 | async-start | bytes 4866048 | tf_op jit(solution)/shard_map/all_gather | solution.py:70
  10.0 317.8 %reduce-scatter.31.cloned.1.call-start = ((), (), s32[]{:S(2)}) async-start(), calls=%async_computation.18 | async-start | bytes 983040
  64.7 11.9 %copy-start.22 = (bf16[2,1,128,768]{3,2,1,0:T(8,128)(2,1)S(1)}, bf16[2,1,128,768]{3,2,1,0:T(8,128)(2,1)}, u32[]{:S(2)}) copy-start(bf16[2,1,128,768]{3,2,1,0:T(8,128)(2,1)} %param.15) | copy-start | bytes 1179652
  73.6 3.2 copy-start.1
  77.7 52.0 %copy-start.42 = (bf16[128,768]{0,1:T(8,128)(2,1)}, bf16[128,768]{0,1:T(8,128)(2,1)S(1)}, u32[]{:S(2)}) copy-start(bf16[128,768]{0,1:T(8,128)(2,1)S(1)} %copy.68) | copy-start | bytes 589828
  260.4 4.0 copy-start.3
  260.4 9.6 %slice-start = ((s8[4718592]{0:T(1024)(128)(4,1)}), s8[4194304]{0:T(1024)(128)(4,1)S(1)}, s32[]{:S(2)}) async-start(s8[4718592]{0:T(1024)(128)(4,1)} %bitcast.187), calls=%async_computation.20 | async-start | bytes 8388608
  264.4 5.6 slice-start.1
  264.4 5.6 copy-start.11
  264.4 5.6 copy-start.54
  264.4 5.6 copy-start.62
  264.5 5.6 copy-start.66
  274.0 7.3 copy-start.25
  295.1 53.6 %reduce-scatter.29.cloned.1.call-start = ((), (), s32[]{:S(2)}) async-start(), calls=%async_computation.17 | async-start | bytes 983040
  296.2 4.3 copy-start.45
  304.1 73.6 %reduce-scatter.27.cloned.1.call-start = ((), (), s32[]{:S(2)}) async-start(), calls=%async_computation.16 | async-start | bytes 983040
  313.4 93.4 %reduce-scatter.25.cloned.1.call-start = ((), (), s32[]{:S(2)}) async-start(), calls=%async_computation.15 | async-start | bytes 983040
  314.6 3.3 copy-start.43
  319.6 193.0 %reduce-scatter.19.cloned.1.call-start = ((), (), s32[]{:S(2)}) async-start(), calls=%async_computation.12 | async-start | bytes 2433024 | tf_op jit(solution)/shard_map/reduce_scatter | solution.py:343
  322.5 3.9 copy-start.9
  322.5 314.8 %reduce-scatter.33.cloned.1.call-start = ((), (), s32[]{:S(2)}) async-start(), calls=%async_computation.19 | async-start | bytes 7299072
  326.4 81.5 %copy-start.24 = (bf16[2,1,128,768]{3,2,1,0:T(8,128)(2,1)S(1)}, bf16[2,1,128,768]{3,2,1,0:T(8,128)(2,1)}, u32[]{:S(2)}) copy-start(bf16[2,1,128,768]{3,2,1,0:T(8,128)(2,1)} %param.15) | copy-start | bytes 1179652
  327.8 81.2 %copy-start.48 = (bf16[12,64,128]{2,1,0:T(8,128)(2,1)}, bf16[12,64,128]{2,1,0:T(8,128)(2,1)S(1)}, u32[]{:S(2)}) copy-start(bf16[12,64,128]{2,1,0:T(8,128)(2,1)S(1)} %get-tuple-element.316) | copy-start | bytes 589828
  328.9 80.1 %copy-start.30 = (bf16[128,768]{0,1:T(8,128)(2,1)}, bf16[128,768]{0,1:T(8,128)(2,1)S(1)}, u32[]{:S(2)}) copy-start(bf16[128,768]{0,1:T(8,128)(2,1)S(1)} %copy.86) | copy-start | bytes 589828
  349.7 59.3 %copy-start.40 = (bf16[128,768]{0,1:T(8,128)(2,1)}, bf16[128,768]{0,1:T(8,128)(2,1)S(1)}, u32[]{:S(2)}) copy-start(bf16[128,768]{0,1:T(8,128)(2,1)S(1)} %copy.84) | copy-start | bytes 589828
  378.8 30.2 %copy-start.35 = (bf16[128,768]{0,1:T(8,128)(2,1)}, bf16[128,768]{0,1:T(8,128)(2,1)S(1)}, u32[]{:S(2)}) copy-start(bf16[128,768]{0,1:T(8,128)(2,1)S(1)} %copy.82) | copy-start | bytes 589828
  421.1 357.8 %reduce-scatter.21.cloned.1.call-start = ((), (), s32[]{:S(2)}) async-start(), calls=%async_computation.13 | async-start | bytes 9732096 | tf_op jit(solution)/shard_map/reduce_scatter | solution.py:343
  428.9 491.4 %reduce-scatter.23.cloned.1.call-start = ((), (), s32[]{:S(2)}) async-start(), calls=%async_computation.14 | async-start | bytes 9732096 | tf_op jit(solution)/shard_map/reduce_scatter | solution.py:343
  436.7 66.8 %copy-start.2 = (bf16[768,2304]{1,0:T(8,128)(2,1)S(1)}, bf16[768,2304]{1,0:T(8,128)(2,1)}, u32[]{:S(2)}) copy-start(bf16[768,2304]{1,0:T(8,128)(2,1)} %all-gather.5.cloned.1.call-done) | copy-start | bytes 10616836
  (52 other events, 93.3 us)
Sparse Core Ops, SparseCore 0:
  10.9 62.6 all-gather.4
  76.5 53.7 all-gather.6
  133.1 62.6 all-gather.8
  198.6 61.8 all-gather.10
  295.2 24.4 reduce-scatter.30
  322.4 26.1 reduce-scatter.28
  351.5 26.1 reduce-scatter.26
  380.6 26.1 reduce-scatter.24
  412.7 99.7 reduce-scatter.18
  518.6 118.6 reduce-scatter.32
  643.8 135.0 reduce-scatter.20
  785.2 135.1 reduce-scatter.22
where the time goes:
time: 934 us; the launch traced here: 928 us
  waiting for transfers between devices  608 us (65%)
  blocking collectives  131 us (14%)
  matrix products  86 us (9%)
  local copies, waits for them, and re-layouts  57.4 us (6%)
  other arithmetic  29.5 us (3%)
  between operations  15.5 us (2%)
    reduce_scatter x3, waiting for transfers between devices, on_device(): lax.psum_scatter(totals, ('dp', 'seq'), scatter_dimension=0, tiled=True)  287 us
    unnamed x17, waiting for transfers between devices  203 us
    unnamed x2, blocking collectives  84.3 us
    all_gather x1, waiting for transfers between devices, gather_forward(): lax.all_gather(shards[8], ('dp', 'seq'), axis=0, tiled=True)  55.9 us
    all_gather x1, waiting for transfers between devices, gather_forward(): lax.all_gather(shards[6], ('dp', 'seq'), axis=0, tiled=True)  52.6 us
    unnamed x177, local copies, waits for them, and re-layouts  46.3 us
    all_gather x2, blocking collectives, on_device(): key_piece = lax.all_gather(keys, 'seq', axis=0, tiled=True)  25.3 us
    dot_general x8, matrix products, matmul(): return jnp.dot(left, right, preferred_element_type=jnp.float32)  24.6 us
  transfers between devices with their start and end apart: 12, of which 10 were waited for; matrix products, arithmetic and copies ran while one was open for 14% of the time, Pallas kernels for 0%

commit v1 on v0

--- a/solution.py
+++ b/solution.py
@@ -178,8 +178,11 @@
             jnp.zeros((HEADS, rows), jnp.float32),
             jnp.zeros((HEADS, rows, head_size), jnp.float32),
         )
-        key_piece = lax.all_gather(keys, "seq", axis=0, tiled=True)
-        value_piece = lax.all_gather(values, "seq", axis=0, tiled=True)
+        key_piece, value_piece = jnp.split(
+            lax.all_gather(jnp.concatenate([keys, values], axis=1), "seq", axis=0, tiled=True),
+            [keys.shape[1]],
+            axis=1,
+        )
         size, count = key_blocks(key_piece.shape[0])
 
         def one(block, carry):

time: 934 us -> 1020 us (1.092)
  local copies, waits for them, and re-layouts: 57.4 us -> 83.4 us
  waiting for transfers between devices: 608 us -> 629 us
  matrix products: 86 us -> 104 us
  blocking collectives: 131 us -> 147 us
    unnamed x17 -> x19, waiting for transfers between devices: 203 us -> 147 us
    all_gather x1, waiting for transfers between devices: 0.01 us -> 46.5 us  [gather_forward(): lax.all_gather(shards[2], ('dp', 'seq'), axis=0, tiled=True)]
    all_gather x0 -> x2, waiting for transfers between devices: none -> 19.6 us  [on_device(): lax.all_gather(jnp.concatenate([keys, values], axis=1), 'seq', axis=0, ti...]
    all_gather x4, blocking collectives: 46.5 us -> 62.6 us  [the longest x2 33.6 us: on_device(): fold_key_piece = lax.all_gather(keys, 'seq', axis=0, tiled=True)]
    split x0 -> x6, local copies, waits for them, and re-layouts: none -> 14.5 us  [on_device(): jnp.split(lax.all_gather(jnp.concatenate([keys, values], axis=1), 'seq',...]
    unnamed x177 -> x179, local copies, waits for them, and re-layouts: 46.3 us -> 49.6 us
  transfers between devices with their start and end apart: 12 -> 14, of which waited for: 10 -> 10; matrix products, arithmetic and copies ran while one was open for 14% -> 17% of each run, Pallas kernels for 0% -> 0%
where the time goes in v1:
time: 1020 us; the launch traced here: 1010 us
  waiting for transfers between devices  629 us (62%)
  blocking collectives  147 us (14%)
  matrix products  104 us (10%)
  local copies, waits for them, and re-layouts  83.4 us (8%)
  other arithmetic  35.6 us (3%)
  between operations  15.1 us (1%)
    reduce_scatter x3, waiting for transfers between devices, on_device(): lax.psum_scatter(totals, ('dp', 'seq'), scatter_dimension=0, tiled=True)  285 us
    unnamed x19, waiting for transfers between devices  147 us
    unnamed x2, blocking collectives  84.4 us
    all_gather x1, waiting for transfers between devices, gather_forward(): lax.all_gather(shards[6], ('dp', 'seq'), axis=0, tiled=True)  58.1 us
    all_gather x1, waiting for transfers between devices, gather_forward(): lax.all_gather(shards[8], ('dp', 'seq'), axis=0, tiled=True)  56.2 us
    unnamed x179, local copies, waits for them, and re-layouts  49.6 us
    all_gather x1, waiting for transfers between devices, gather_forward(): lax.all_gather(shards[2], ('dp', 'seq'), axis=0, tiled=True)  46.5 us
    all_gather x2, blocking collectives, on_device(): fold_key_piece = lax.all_gather(keys, 'seq', axis=0, tiled=True)  33.6 us
  transfers between devices with their start and end apart: 14, of which 10 were waited for; matrix products, arithmetic and copies ran while one was open for 17% of the time, Pallas kernels for 0%

profile of v1, /device:TPU:0, one launch (start us, length us, event | category | flops | bytes accessed | tf_op | source)
XLA Modules:
  0.0 1014.5 jit_solution(15896169749843315307)
XLA Ops:
  14.7 42.8 %all-reduce.17 = (bf16[3072]{0:T(1024)(128)(2,1)}, bf16[1536]{0:T(1024)(128)(2,1)S(1)}, bf16[768]{0:T(1024)(128)(2,1)}, bf16[768]{0:T(1024)(128)(2,1)}, bf16[768...) all-reduce(bf16[3072]{0:T(1024)(128)(2,1)S(1)} %dynamic-update-slic, ...), channel_id=1, replica_groups=mesh['dp'=8,'seq'=4] {'dp','seq'}, use_global_device_ids=true, to_apply=%add.4 | all-reduce | flops 9216 | bytes 36864
  57.5 16.2 %all-gather.7.cloned.1.call-done = bf16[768,2304]{1,0:T(8,128)(2,1)} async-done(((bf16[24,2304]{1,0:T(8,128)(2,1)}), bf16[768,2304]{1,0:T(8,128)(2,1)}) %all-gather.7.cloned.1.call-update) | async-done | bytes 3538960 | tf_op jit(solution)/shard_map/all_gather | solution.py:62
  97.1 19.7 %all_gather.90 = bf16[512,768]{1,0:T(8,128)(2,1)} all-gather(bf16[128,768]{1,0:T(8,128)(2,1)} %copy-done.43), channel_id=1, replica_groups=mesh['dp'=8,'seq'=4] {'seq'}, dimensions={0}, use_global_device_ids=true | all-gather | bytes 983040 | tf_op jit(solution)/shard_map/all_gather | solution.py:259
  119.1 3.5 fusion.167
  129.8 19.6 %all-gather.17.cloned.1.call-done = bf16[512,1536]{1,0:T(8,128)(2,1)} async-done(((bf16[128,1536]{1,0:T(8,128)(2,1)}), bf16[512,1536]{1,0:T(8,128)(2,1)}) %all-gather.17.cloned.1.call-update) | async-done | bytes 1572880 | tf_op jit(solution)/shard_map/all_gather | solution.py:182
  159.8 46.5 %all-gather.11.cloned.1.call-done = bf16[768,768]{1,0:T(8,128)(2,1)} async-done(((bf16[24,768]{1,0:T(8,128)(2,1)}), bf16[768,768]{1,0:T(8,128)(2,1)}) %all-gather.11.cloned.1.call-update) | async-done | bytes 1179664 | tf_op jit(solution)/shard_map/all_gather | solution.py:64
  213.3 58.1 %all-gather.13.cloned.1.call-done = bf16[768,3072]{1,0:T(8,128)(2,1)} async-done(((bf16[24,3072]{1,0:T(8,128)(2,1)}), bf16[768,3072]{1,0:T(8,128)(2,1)}) %all-gather.13.cloned.1.call-update) | async-done | bytes 4718608 | tf_op jit(solution)/shard_map/all_gather | solution.py:68
  271.4 8.5 multiply_convert_fusion.5
  279.9 56.2 %all-gather.15.cloned.1.call-done = bf16[3072,768]{1,0:T(8,128)(2,1)} async-done(((bf16[96,768]{1,0:T(8,128)(2,1)}), bf16[3072,768]{1,0:T(8,128)(2,1)}) %all-gather.15.cloned.1.call-update) | async-done | bytes 4718608 | tf_op jit(solution)/shard_map/all_gather | solution.py:70
  336.1 3.5 fusion.162
  343.4 4.2 fusion.163
  348.5 4.2 multiply_convert_fusion.4
  364.1 3.5 convert_reduce_fusion.7
  372.2 3.7 fusion.47
  378.4 16.3 %all_gather.91 = bf16[512,768]{1,0:T(8,128)(2,1)} all-gather(bf16[128,768]{1,0:T(8,128)(2,1)} %get-tuple-element.275), channel_id=1, replica_groups=mesh['dp'=8,'seq'=4] {'seq'}, dimensions={0}, use_global_device_ids=true | all-gather | bytes 983040 | tf_op jit(solution)/shard_map/all_gather | solution.py:260
  398.1 3.4 multiply_convert_fusion
  406.4 13.9 %all_gather.88 = bf16[512,768]{1,0:T(8,128)(2,1)} all-gather(bf16[128,768]{1,0:T(8,128)(2,1)} %copy-done.42), channel_id=1, replica_groups=mesh['dp'=8,'seq'=4] {'seq'}, dimensions={0}, use_global_device_ids=true | all-gather | bytes 983040 | tf_op jit(solution)/shard_map/all_gather | solution.py:259
  422.7 3.6 fusion.166
  429.3 3.9 fusion.44
  435.6 12.7 %all_gather.89 = bf16[512,768]{1,0:T(8,128)(2,1)} all-gather(bf16[128,768]{1,0:T(8,128)(2,1)} %copy-done.41), channel_id=1, replica_groups=mesh['dp'=8,'seq'=4] {'seq'}, dimensions={0}, use_global_device_ids=true | all-gather | bytes 983040 | tf_op jit(solution)/shard_map/all_gather | solution.py:260
  451.7 3.4 multiply_convert_fusion.1
  463.7 3.2 convert_reduce_fusion.9
  474.0 19.8 %reduce-scatter.25.cloned.1.call-done = bf16[128,768]{1,0:T(8,128)(2,1)} async-done(((bf16[512,768]{1,0:T(8,128)(2,1)}), bf16[128,768]{1,0:T(8,128)(2,1)}) %reduce-scatter.25.cloned.1.call-update) | async-done | bytes 196624
  497.9 4.0 add_bitcast_fusion
  501.9 8.1 copy.103
  510.1 2.9 fusion.151
  513.0 5.1 convolution_add_fusion.1
  521.0 5.1 convolution_add_fusion
  540.9 41.6 %all-reduce.16 = (f32[1536]{0:T(1024)}, f32[768]{0:T(1024)}, f32[768]{0:T(1024)}, f32[768]{0:T(1024)}, f32[3072]{0:T(1024)}, /*index=5*/f32[768]{0:T(1024)}, f32[768]{0:T(1024)}, f32[768]{0:T(1024)}) all-reduce(f32[1536]{0:T(1024)} %maximum_add_fusion, f32[768]{0:T(1024)S(1)} %add.424, ...), channel_id=7, replica_groups=mesh['dp'=8,'seq'=4] {'dp','seq'}, use_global_device_ids=true, to_apply=%region_35.36.clone | all-reduce | flops 9216 | bytes 73728
  599.4 124.8 %reduce-scatter.33.cloned.1.call-done = f32[24,2304]{1,0:T(8,128)} async-done(((f32[768,2304]{1,0:T(8,128)}), f32[24,2304]{1,0:T(8,128)}) %reduce-scatter.33.cloned.1.call-update) | async-done | bytes 221200
  724.2 141.7 %reduce-scatter.21.cloned.1.call-done = f32[24,3072]{1,0:T(8,128)} async-done(((f32[768,3072]{1,0:T(8,128)}), f32[24,3072]{1,0:T(8,128)}) %reduce-scatter.21.cloned.1.call-update) | async-done | bytes 294928 | tf_op jit(solution)/shard_map/reduce_scatter | solution.py:346
  865.9 141.8 %reduce-scatter.23.cloned.1.call-done = f32[96,768]{1,0:T(8,128)} async-done(((f32[3072,768]{1,0:T(8,128)}), f32[96,768]{1,0:T(8,128)}) %reduce-scatter.23.cloned.1.call-update) | async-done | bytes 294928 | tf_op jit(solution)/shard_map/reduce_scatter | solution.py:346
  (317 shorter events, 154.0 us)
Async XLA Ops:
  7.2 66.5 %all-gather.7.cloned.1.call-start = ((), (), s32[]{:S(2)}) async-start(), calls=%async_computation.8 | async-start | bytes 3649536 | tf_op jit(solution)/shard_map/all_gather | solution.py:62
  7.9 114.7 %all-gather.9.cloned.1.call-start = ((), (), s32[]{:S(2)}) async-start(), calls=%async_computation.9 | async-start | bytes 1966080 | tf_op jit(solution)/shard_map/all_gather | solution.py:182
  79.4 7.4 copy-start.63
  80.9 68.6 %all-gather.17.cloned.1.call-start = ((), (), s32[]{:S(2)}) async-start(), calls=%async_computation.13 | async-start | bytes 1966080 | tf_op jit(solution)/shard_map/all_gather | solution.py:182
  84.4 121.9 %all-gather.11.cloned.1.call-start = ((), (), s32[]{:S(2)}) async-start(), calls=%async_computation.10 | async-start | bytes 1216512 | tf_op jit(solution)/shard_map/all_gather | solution.py:64
  85.0 186.4 %all-gather.13.cloned.1.call-start = ((), (), s32[]{:S(2)}) async-start(), calls=%async_computation.11 | async-start | bytes 4866048 | tf_op jit(solution)/shard_map/all_gather | solution.py:68
  85.5 250.5 %all-gather.15.cloned.1.call-start = ((), (), s32[]{:S(2)}) async-start(), calls=%async_computation.12 | async-start | bytes 4866048 | tf_op jit(solution)/shard_map/all_gather | solution.py:70
  86.1 382.6 %reduce-scatter.31.cloned.1.call-start = ((), (), s32[]{:S(2)}) async-start(), calls=%async_computation.20 | async-start | bytes 983040
  343.4 5.0 slice-start
  343.4 4.3 copy-start.1
  343.4 4.3 copy-start.20
  343.4 4.3 copy-start.49
  343.4 5.0 slice-start.1
  347.7 4.9 slice-start.2
  348.2 19.5 %copy-start.5 = (f32[128,768]{1,0:T(8,128)}, f32[128,768]{1,0:T(8,128)S(1)}, u32[]{:S(2)}) copy-start(f32[128,768]{1,0:T(8,128)S(1)} %get-tuple-element.313) | copy-start | bytes 1179652
  348.2 19.5 %copy-start.55 = (f32[128]{0:T(128)}, f32[128]{0:T(128)S(1)}, u32[]{:S(2)}) copy-start(f32[128]{0:T(128)S(1)} %broadcast_multiply_fusion.9) | copy-start | bytes 1540
  348.5 19.2 %copy-start.59 = (f32[128]{0:T(128)}, f32[128]{0:T(128)S(1)}, u32[]{:S(2)}) copy-start(f32[128]{0:T(128)S(1)} %add_rsqrt_fusion.1) | copy-start | bytes 1540
  348.5 4.2 slice-start.3
  356.8 7.3 copy-start.22
  364.1 3.5 copy-start.29
  367.7 4.5 copy-start.62
  378.3 92.2 %reduce-scatter.29.cloned.1.call-start = ((), (), s32[]{:S(2)}) async-start(), calls=%async_computation.19 | async-start | bytes 983040
  398.1 4.6 copy-start.33
  406.3 65.9 %reduce-scatter.27.cloned.1.call-start = ((), (), s32[]{:S(2)}) async-start(), calls=%async_computation.18 | async-start | bytes 983040
  422.7 3.7 copy-start.2
  422.7 3.7 copy-start.9
  435.5 58.2 %reduce-scatter.25.cloned.1.call-start = ((), (), s32[]{:S(2)}) async-start(), calls=%async_computation.17 | async-start | bytes 983040
  451.7 4.5 copy-start.31
  459.8 139.6 %reduce-scatter.19.cloned.1.call-start = ((), (), s32[]{:S(2)}) async-start(), calls=%async_computation.14 | async-start | bytes 2433024 | tf_op jit(solution)/shard_map/reduce_scatter | solution.py:346
  463.4 260.8 %reduce-scatter.33.cloned.1.call-start = ((), (), s32[]{:S(2)}) async-start(), calls=%async_computation.21 | async-start | bytes 7299072
  510.0 356.0 %reduce-scatter.21.cloned.1.call-start = ((), (), s32[]{:S(2)}) async-start(), calls=%async_computation.15 | async-start | bytes 9732096 | tf_op jit(solution)/shard_map/reduce_scatter | solution.py:346
  518.2 489.6 %reduce-scatter.23.cloned.1.call-start = ((), (), s32[]{:S(2)}) async-start(), calls=%async_computation.16 | async-start | bytes 9732096 | tf_op jit(solution)/shard_map/reduce_scatter | solution.py:346
  (55 other events, 114.1 us)
Sparse Core Ops, SparseCore 0:
  10.9 62.7 all-gather.6
  81.0 35.2 all-gather.8
  118.1 31.2 all-gather.16
  152.2 53.9 all-gather.10
  209.0 62.3 all-gather.12
  274.1 61.8 all-gather.14
  378.5 26.6 reduce-scatter.30
  408.0 27.2 reduce-scatter.28
  438.3 26.5 reduce-scatter.26
  467.6 26.1 reduce-scatter.24
  499.6 99.7 reduce-scatter.18
  605.5 118.6 reduce-scatter.32
  730.7 135.2 reduce-scatter.20
  872.3 135.4 reduce-scatter.22
